TPU v7x, 32 devices: a whole 2x2x4 slice. The times are simulated.
32 devices in a mesh: blk: 16 (over z, y, x), sub: 2 (over core).
Axes of the slice: x: 2, y: 2, z: 4, core: 2. Of those that a mesh axis runs over, the one named last changes fastest.
Arguments:
- normal_wind: float32 [32, 55, 768], P(('blk', 'sub')), may hold values from -6 to 6
- density: float32 [32, 55, 256], P(('blk', 'sub')), may hold values from 0.5 to 1.5
- theta_field: float32 [32, 55, 256], P(('blk', 'sub')), may hold values from -6 to 6
- cell_edges: int32 [32, 6, 256], P(('blk', 'sub')), may hold values from 0 to 1663, as said below
- edge_cells: int32 [32, 2, 1664], P(('blk', 'sub')), may hold values from 0 to 703, as said below
- edges_on_edge: int32 [32, 10, 768], P(('blk', 'sub')), may hold values from 0 to 1663, as said below
- send_cells: int32 [32, 7, 64], P(('blk', 'sub')), may hold values from 0 to 255
- send_edges: int32 [32, 7, 128], P(('blk', 'sub')), may hold values from 0 to 767
- cell_weight: float32 [32, 6, 256], P(('blk', 'sub')), may hold values from -4 to 4
- eoe_weight: float32 [32, 10, 768], P(('blk', 'sub')), may hold values from -2 to 2
- vert_coupling: float32 [32, 54, 256], P(('blk', 'sub')), may hold values from 0.05 to 4
Outputs:
- density_tend: float32 [32, 55, 256], P(('blk', 'sub'))
- theta_new: float32 [32, 55, 256], P(('blk', 'sub'))
- tangential_wind: float32 [32, 55, 768], P(('blk', 'sub'))
Inputs may be any that keep to these rules, and one draw needn't show every extreme that they name: `cell_edges`: positions in the block's extended edge list: owned edges, then 128 received edges for each slot in order. `edge_cells`: positions in the block's extended cell list: owned cells, then 64 received cells for each slot in order. `edges_on_edge`: positions in the block's extended edge list.
All inputs are finite; a program needn't handle non-finite values.
Results may differ from a plain program's by a relative error of at most 0.0003.
Values sent between devices are 32-bit elements; how exact they have to be, the bound alone decides.
A program may use at most 64 MiB of HBM per device.

v0:
```python
import functools

import jax
import jax.numpy as jnp
from jax import lax
from jax.experimental import pallas as pl
from jax.experimental.pallas import tpu as pltpu
from jax.sharding import PartitionSpec as P

STEP_SIZE = 0.2
OFFSETS = (1, -1, 2, -2, 3, -3)
SEND_ORDER = (4, 5, 2, 3, 0, 1, 6)
LANES = 128
F32 = jnp.float32
BF16 = jnp.bfloat16


def halves(values):
    lead = values.astype(BF16).astype(F32)
    return jnp.concatenate([lead, values - lead], axis=0).astype(BF16)


def dot(left, right):
    return jnp.dot(left, right, preferred_element_type=F32)


def merged_weights(indices, weights):
    total = jnp.zeros_like(weights)
    for term in range(indices.shape[0]):
        total = total + jnp.where(
            indices == indices[term : term + 1], weights[term : term + 1], 0.0
        )
    return total


def build(index_ref, weight_ref, lead_ref, trail_ref):
    terms = weight_ref.shape[0]
    row_tiles = lead_ref.shape[0] // LANES
    column_tiles = lead_ref.shape[1] // LANES

    def tile(step, carry):
        row = pl.multiple_of(lax.rem(step, row_tiles) * LANES, LANES)
        column = pl.multiple_of(lax.div(step, row_tiles) * LANES, LANES)
        columns = pl.ds(column, LANES)
        positions = lax.broadcasted_iota(jnp.int32, (LANES, LANES), 0) + row
        matrix = jnp.zeros((LANES, LANES), F32)
        for term in range(terms):
            matrix = jnp.where(
                positions == index_ref[term : term + 1, columns],
                weight_ref[term : term + 1, columns],
                matrix,
            )
        lead = matrix.astype(BF16)
        lead_ref[pl.ds(row, LANES), columns] = lead
        if trail_ref is not None:
            trail_ref[pl.ds(row, LANES), columns] = (matrix - lead.astype(F32)).astype(BF16)
        return carry

    lax.fori_loop(0, row_tiles * column_tiles, tile, 0)


def spread(indices, weights, index_ref, lead_ref, trail_ref):
    terms, outputs = indices.shape
    rows = index_ref.shape[1]
    lead = weights.astype(BF16).astype(F32)
    for term in range(terms):
        def tiled(table):
            return jnp.broadcast_to(table[term : term + 1], (rows, outputs))

        index_ref[term] = tiled(indices).astype(jnp.int16)
        lead_ref[term] = tiled(lead).astype(BF16)
        if trail_ref is not None:
            trail_ref[term] = tiled(weights - lead).astype(BF16)


def build_packed(chunk, place_ref, tables, lead_out, trail_out):
    index_ref, lead_ref, trail_ref = tables
    terms, rows = index_ref.shape[:2]
    row_tiles = lead_out.shape[0] // chunk
    column_tiles = lead_out.shape[1] // LANES

    def tile(step, carry):
        row = pl.multiple_of(lax.rem(step, row_tiles) * chunk, chunk)
        column = pl.multiple_of(lax.div(step, row_tiles) * LANES, LANES)
        columns = pl.ds(column, LANES)
        zero = jnp.zeros((rows, LANES), BF16)
        indices = [index_ref[term, :, columns] for term in range(terms)]
        leads = [lead_ref[term, :, columns] for term in range(terms)]
        if trail_out is not None:
            trails = [trail_ref[term, :, columns] for term in range(terms)]
        for part in range(chunk // rows):
            here = pl.ds(row + part * rows, rows)
            places = place_ref[here, :]
            lead, trail = zero, zero
            for term in range(terms):
                hit = places == indices[term]
                lead = jnp.where(hit, leads[term], lead)
                if trail_out is not None:
                    trail = jnp.where(hit, trails[term], trail)
            lead_out[here, columns] = lead
            if trail_out is not None:
                trail_out[here, columns] = trail
        return carry

    lax.fori_loop(0, row_tiles * column_tiles, tile, 0)


def kernel(
    wind_hbm, density_hbm, theta_hbm, cell_edges_hbm, edge_cells_hbm, edges_on_edge_hbm,
    send_cells_hbm, send_edges_hbm, cell_weight_hbm, eoe_weight_hbm, coupling_hbm,
    tend_hbm, theta_new_hbm, tangential_hbm,
    wind_ref, density_ref, theta_ref,
    cell_edges_ref, edge_cells_ref, edges_on_edge_ref, send_cells_ref, send_edges_ref,
    cell_weight_ref, eoe_weight_ref, coupling_ref, tend_ref, theta_new_ref, tangential_ref,
    wind_ext, density_ext, theta_ext, send, received,
    average, average_index, average_lead, places, diverge, diverge_trail, diverge_weight,
    tangent, tangent_trail, tangent_weight,
    average_sum, tangent_sum, inverse, carried, ratios, values,
    send_sem, recv_sem, load_sem, store_sem,
):
    blocks = lax.axis_size("blk")
    position = lax.axis_index("blk")
    side = lax.axis_index("sub")
    levels, edges = tangential_ref.shape
    cells = tend_ref.shape[1]
    slots, halo_cells = send_cells_ref.shape
    halo_edges = send_edges_ref.shape[1]
    padded = wind_ext.shape[0]

    def target(slot):
        if slot < len(OFFSETS):
            return (lax.rem(position + OFFSETS[slot] + blocks, blocks), side)
        return (position, 1 - side)

    loads = (
        (send_edges_hbm, send_edges_ref),
        (wind_hbm, wind_ref),
        (send_cells_hbm, send_cells_ref),
        (density_hbm, density_ref),
        (theta_hbm, theta_ref),
        (edge_cells_hbm, edge_cells_ref),
        (cell_edges_hbm, cell_edges_ref),
        (cell_weight_hbm, cell_weight_ref),
        (edges_on_edge_hbm, edges_on_edge_ref),
        (eoe_weight_hbm, eoe_weight_ref),
        (coupling_hbm, coupling_ref),
    )
    loads = [
        pltpu.make_async_copy(
            source.at[0] if source is edge_cells_hbm else source.at[:, 0, :], target_ref, load_sem.at[n]
        )
        for n, (source, target_ref) in enumerate(loads)
    ]
    for load in loads:
        load.start()

    barrier = pltpu.get_barrier_semaphore()
    for slot in range(slots):
        pl.semaphore_signal(
            barrier, inc=1, device_id=target(slot), device_id_type=pl.DeviceIdType.MESH
        )

    for load in loads[:5]:
        load.wait()
    for ext, ref in ((wind_ext, wind_ref), (density_ext, density_ref), (theta_ext, theta_ref)):
        owned = ref.shape[1]
        ext[0:levels, 0:owned] = ref[...]
        if levels < padded:
            ext[levels:padded, 0:owned] = jnp.zeros((padded - levels, owned), F32)
    spare = cells + slots * halo_cells
    for ext in (density_ext, theta_ext):
        if spare < ext.shape[1]:
            ext[:, spare:] = jnp.zeros((padded, ext.shape[1] - spare), F32)

    wind_own = halves(wind_ext[:, 0:edges])
    cells_own = halves(
        jnp.concatenate([density_ext[:, 0:cells], theta_ext[:, 0:cells]], axis=0)
    )

    edge_rows = lax.broadcasted_iota(jnp.int32, (edges, halo_edges), 0)
    cell_rows = lax.broadcasted_iota(jnp.int32, (cells, halo_cells), 0)
    for slot in range(slots):
        picks = jnp.where(edge_rows == send_edges_ref[slot : slot + 1, :], 1.0, 0.0).astype(BF16)
        both = dot(wind_own, picks)
        send[slot, :, 2 * halo_cells :] = both[0:padded] + both[padded:]
        picks = jnp.where(cell_rows == send_cells_ref[slot : slot + 1, :], 1.0, 0.0).astype(BF16)
        both = dot(cells_own, picks)
        both = both[0 : 2 * padded] + both[2 * padded :]
        send[slot, :, 0:halo_cells] = both[0:padded]
        send[slot, :, halo_cells : 2 * halo_cells] = both[padded:]

    def copy_of(slot):
        return pltpu.make_async_remote_copy(
            src_ref=send.at[slot],
            dst_ref=received.at[slot],
            send_sem=send_sem.at[slot],
            recv_sem=recv_sem.at[slot],
            device_id=target(slot),
            device_id_type=pl.DeviceIdType.MESH,
        )

    pl.semaphore_wait(barrier, slots)
    for slot in SEND_ORDER:
        copy_of(slot).start()

    for load in loads[5:]:
        load.wait()
    tangent_weight[...] = merged_weights(edges_on_edge_ref[...], eoe_weight_ref[...])
    diverge_weight[...] = merged_weights(cell_edges_ref[...], cell_weight_ref[...])
    average_tables = (average_index, average_lead, None)
    spread(
        edge_cells_ref[...],
        merged_weights(edge_cells_ref[...], jnp.full(edge_cells_ref.shape, 0.5, F32)),
        *average_tables,
    )
    places[...] = lax.broadcasted_iota(jnp.int32, places.shape, 0).astype(jnp.int16)
    build_packed(average.shape[0], places, average_tables, average, None)
    build(cell_edges_ref, diverge_weight, diverge, diverge_trail)
    build(edges_on_edge_ref, tangent_weight, tangent, tangent_trail)

    ratio = jnp.zeros((1, cells), F32)
    below = jnp.zeros((1, cells), F32)
    for level in range(levels):
        if level < levels - 1:
            above = coupling_ref[level : level + 1, :]
        else:
            above = jnp.zeros((1, cells), F32)
        reciprocal = 1.0 / (1.0 + below + above - below * ratio)
        ratio = above * reciprocal
        inverse[level : level + 1, :] = reciprocal
        carried[level : level + 1, :] = below * reciprocal
        ratios[level : level + 1, :] = ratio
        below = above

    wind_own = halves(wind_ext[:, 0:edges])
    both = dot(wind_own, tangent[0:edges, :])
    tangent_sum[...] = both[0:padded] + both[padded:] + dot(
        wind_own[0:padded], tangent_trail[0:edges, :]
    )
    own = density_ext[:, 0:cells]
    both = dot(
        halves(jnp.concatenate([own, own * theta_ext[:, 0:cells]], axis=0)),
        average[0:cells, :],
    )
    average_sum[...] = both[0 : 2 * padded] + both[2 * padded :]

    for slot in SEND_ORDER:
        copy_of(slot).wait_recv()
    for slot in range(slots):
        start = cells + slot * halo_cells
        density_ext[:, start : start + halo_cells] = received[slot, :, 0:halo_cells]
        theta_ext[:, start : start + halo_cells] = received[slot, :, halo_cells : 2 * halo_cells]
        start = edges + slot * halo_edges
        wind_ext[:, start : start + halo_edges] = received[slot, :, 2 * halo_cells :]

    halo = density_ext[:, cells:]
    both = dot(
        halves(jnp.concatenate([halo, halo * theta_ext[:, cells:]], axis=0)),
        average[cells:, :],
    )
    averaged = average_sum[...] + both[0 : 2 * padded] + both[2 * padded :]
    wind = wind_ext[...]
    fluxes = halves(jnp.concatenate([wind, wind], axis=0) * averaged)
    both = dot(fluxes, diverge[...])
    divergence = both[0 : 2 * padded] + both[2 * padded :] + dot(
        fluxes[0 : 2 * padded], diverge_trail[...]
    )
    tend_ref[...] = -divergence[0:levels]
    stores = [
        pltpu.make_async_copy(source, target_ref.at[:, 0, :], store_sem.at[n])
        for n, (source, target_ref) in enumerate(
            ((tend_ref, tend_hbm), (tangential_ref, tangential_hbm), (theta_new_ref, theta_new_hbm))
        )
    ]
    values[...] = (theta_ext[:, 0:cells] - STEP_SIZE * divergence[padded:])
    values[0:levels, :] = values[0:levels, :] * inverse[0:levels, :]

    wind_halo = halves(wind_ext[:, edges:])
    both = dot(wind_halo, tangent[edges:, :])
    tangential = tangent_sum[...] + both[0:padded] + both[padded:] + dot(
        wind_halo[0:padded], tangent_trail[edges:, :]
    )
    tangential_ref[...] = tangential[0:levels]
    stores[0].start()

    value = jnp.zeros((1, cells), F32)
    for level in range(levels):
        value = values[level : level + 1, :] + carried[level : level + 1, :] * value
        values[level : level + 1, :] = value
    theta_new_ref[levels - 1 : levels, :] = value
    for level in range(levels - 2, -1, -1):
        value = values[level : level + 1, :] + ratios[level : level + 1, :] * value
        theta_new_ref[level : level + 1, :] = value
        if level == levels // 2:
            stores[1].start()
    stores[2].start()
    for store in stores:
        store.wait()

    for slot in SEND_ORDER:
        copy_of(slot).wait_send()


def spread_of(table):
    shape = (table.shape[1], 16, table.shape[2])
    return [pltpu.VMEM(shape, kind) for kind in (jnp.int16, BF16, BF16)]


def shards(*arguments):
    wind, density, theta, cell_edges, edge_cells, edges_on_edge, send_cells, send_edges = arguments[:8]
    levels, edges = wind.shape[1:]
    cells = density.shape[2]
    slots, halo_cells = send_cells.shape[1:]
    halo_edges = send_edges.shape[2]
    padded = -(-levels // 8) * 8
    edges_ext = edge_cells.shape[2]
    cells_ext = -(-(cells + slots * halo_cells) // LANES) * LANES
    landed = [*arguments[:3], cell_edges, edge_cells, edges_on_edge, send_cells, send_edges, *arguments[8:]]
    operands = [x if x is edge_cells else jnp.transpose(x, (1, 0, 2)) for x in arguments]
    hbm = pl.BlockSpec(memory_space=pl.ANY)
    results = pl.pallas_call(
        kernel,
        out_shape=(
            jax.ShapeDtypeStruct((levels, 1, cells), F32),
            jax.ShapeDtypeStruct((levels, 1, cells), F32),
            jax.ShapeDtypeStruct((levels, 1, edges), F32),
        ),
        in_specs=[hbm] * len(arguments),
        out_specs=(hbm,) * 3,
        scratch_shapes=[
            *(pltpu.VMEM(x.shape[1:], x.dtype) for x in landed),
            pltpu.VMEM((levels, cells), F32),
            pltpu.VMEM((levels, cells), F32),
            pltpu.VMEM((levels, edges), F32),
            pltpu.VMEM((padded, edges_ext), F32),
            pltpu.VMEM((padded, cells_ext), F32),
            pltpu.VMEM((padded, cells_ext), F32),
            pltpu.VMEM((slots, padded, 2 * halo_cells + halo_edges), F32),
            pltpu.VMEM((slots, padded, 2 * halo_cells + halo_edges), F32),
            pltpu.VMEM((cells_ext, edges_ext), BF16),
            *spread_of(edge_cells)[:2],
            pltpu.VMEM((cells_ext, LANES), jnp.int16),
            pltpu.VMEM((edges_ext, cells), BF16),
            pltpu.VMEM((edges_ext, cells), BF16),
            pltpu.VMEM(cell_edges.shape[1:], F32),
            pltpu.VMEM((edges_ext, edges), BF16),
            pltpu.VMEM((edges_ext, edges), BF16),
            pltpu.VMEM(edges_on_edge.shape[1:], F32),
            pltpu.VMEM((2 * padded, edges_ext), F32),
            pltpu.VMEM((padded, edges), F32),
            pltpu.VMEM((padded, cells), F32),
            pltpu.VMEM((padded, cells), F32),
            pltpu.VMEM((padded, cells), F32),
            pltpu.VMEM((padded, cells), F32),
            pltpu.SemaphoreType.DMA((slots,)),
            pltpu.SemaphoreType.DMA((slots,)),
            pltpu.SemaphoreType.DMA((len(arguments),)),
            pltpu.SemaphoreType.DMA((3,)),
        ],
        compiler_params=pltpu.CompilerParams(collective_id=0, has_side_effects=True),
    )(*operands)
    return tuple(jnp.transpose(x, (1, 0, 2)) for x in results)


def solution(mesh):
    placed = P(("blk", "sub"), None, None)
    return jax.shard_map(
        shards,
        mesh=mesh,
        in_specs=(placed,) * 11,
        out_specs=(placed,) * 3,
        check_vma=False,
    )
```

profile of v0, /device:TPU:0, one launch (start us, length us, event | category | flops | bytes accessed | tf_op | source)
XLA Modules:
  0.0 22.1 jit_solution(15440683410757481324)
XLA Ops:
  0.6 17.8 %shard_map.130 = (f32[55,1,256]{2,1,0:T(1,128)}, f32[55,1,256]{2,1,0:T(1,128)}, f32[55,1,768]{2,1,0:T(1,128)}) custom-call(f32[55,1,768]{2,1,0:T(1,128)} %bitcast.13, f32[55,1,256]{2,1,0:T(1,128)} %bitcast.17, f32[55,1,256]{2,1,0:T(1,128)} %bitcast.18, s32[6,1,256]{2,1,0:T(1,128)} %bitcast.22, s32[1,2,1664]{2,1,0:T(2,128)} %edge_cells_hbm.1, ...), custom_call_target="tpu_custom_call" | custom-call | tf_op jit(solution)/shard_map/pallas_call | solution.py:321
  18.5 0.0 copy-start
  18.5 1.5 %copy.17 = f32[1,55,256]{2,0,1:T(1,128)} copy(f32[1,55,256]{2,0,1:T(1,128)} %bitcast.16) | data formatting | bytes 112640
  19.9 1.4 %copy.18 = f32[1,55,256]{2,0,1:T(1,128)} copy(f32[1,55,256]{2,0,1:T(1,128)} %bitcast.15) | data formatting | bytes 112640
  21.4 0.0 copy-done
  21.4 0.7 %copy.19 = f32[1,55,768]{2,0,1:T(1,128)} copy(f32[1,55,768]{2,0,1:T(1,128)S(1)} %bitcast.14) | data formatting | bytes 337920
Async XLA Ops:
  18.5 2.9 %copy-start = (f32[55,1,768]{2,1,0:T(1,128)S(1)}, f32[55,1,768]{2,1,0:T(1,128)}, u32[]{:S(2)}) copy-start(f32[55,1,768]{2,1,0:T(1,128)} %get-tuple-element.8) | copy-start | bytes 506884
where the time goes:
time: 22.3 us; the launch traced here: 22.1 us
  Pallas kernels  17.8 us (80%)
  local copies, waits for them, and re-layouts  3.6 us (16%)
  between operations  0.65 us (3%)
    pallas_call x1, Pallas kernels, shards(): pl.pallas_call(kernel, out_shape=(jax.ShapeDtypeStruct((levels, 1, cells)...  17.8 us
    unnamed x5, local copies, waits for them, and re-layouts  3.6 us

commit v1 on v0

--- a/solution.py
+++ b/solution.py
@@ -108,15 +108,15 @@
 def kernel(
     wind_hbm, density_hbm, theta_hbm, cell_edges_hbm, edge_cells_hbm, edges_on_edge_hbm,
     send_cells_hbm, send_edges_hbm, cell_weight_hbm, eoe_weight_hbm, coupling_hbm,
-    tend_hbm, theta_new_hbm, tangential_hbm,
+    tend_ref, theta_new_ref, tangential_ref,
     wind_ref, density_ref, theta_ref,
     cell_edges_ref, edge_cells_ref, edges_on_edge_ref, send_cells_ref, send_edges_ref,
-    cell_weight_ref, eoe_weight_ref, coupling_ref, tend_ref, theta_new_ref, tangential_ref,
+    cell_weight_ref, eoe_weight_ref, coupling_ref,
     wind_ext, density_ext, theta_ext, send, received,
     average, average_index, average_lead, places, diverge, diverge_trail, diverge_weight,
     tangent, tangent_trail, tangent_weight,
     average_sum, tangent_sum, inverse, carried, ratios, values,
-    send_sem, recv_sem, load_sem, store_sem,
+    send_sem, recv_sem, load_sem,
 ):
     blocks = lax.axis_size("blk")
     position = lax.axis_index("blk")
@@ -266,12 +266,6 @@
         fluxes[0 : 2 * padded], diverge_trail[...]
     )
     tend_ref[...] = -divergence[0:levels]
-    stores = [
-        pltpu.make_async_copy(source, target_ref.at[:, 0, :], store_sem.at[n])
-        for n, (source, target_ref) in enumerate(
-            ((tend_ref, tend_hbm), (tangential_ref, tangential_hbm), (theta_new_ref, theta_new_hbm))
-        )
-    ]
     values[...] = (theta_ext[:, 0:cells] - STEP_SIZE * divergence[padded:])
     values[0:levels, :] = values[0:levels, :] * inverse[0:levels, :]
 
@@ -281,7 +275,6 @@
         wind_halo[0:padded], tangent_trail[edges:, :]
     )
     tangential_ref[...] = tangential[0:levels]
-    stores[0].start()
 
     value = jnp.zeros((1, cells), F32)
     for level in range(levels):
@@ -291,14 +284,21 @@
     for level in range(levels - 2, -1, -1):
         value = values[level : level + 1, :] + ratios[level : level + 1, :] * value
         theta_new_ref[level : level + 1, :] = value
-        if level == levels // 2:
-            stores[1].start()
-    stores[2].start()
+
+    for slot in SEND_ORDER:
+        copy_of(slot).wait_send()
+
+
+def deliver(*refs):
+    sources, targets, store_sem = refs[:3], refs[3:6], refs[6]
+    stores = [
+        pltpu.make_async_copy(source, target_ref.at[:, 0, :], store_sem.at[n])
+        for n, (source, target_ref) in enumerate(zip(sources, targets))
+    ]
+    for store in stores:
+        store.start()
     for store in stores:
         store.wait()
-
-    for slot in SEND_ORDER:
-        copy_of(slot).wait_send()
 
 
 def spread_of(table):
@@ -318,20 +318,15 @@
     landed = [*arguments[:3], cell_edges, edge_cells, edges_on_edge, send_cells, send_edges, *arguments[8:]]
     operands = [x if x is edge_cells else jnp.transpose(x, (1, 0, 2)) for x in arguments]
     hbm = pl.BlockSpec(memory_space=pl.ANY)
+    vmem = pl.BlockSpec(memory_space=pltpu.VMEM)
+    widths = (cells, cells, edges)
     results = pl.pallas_call(
         kernel,
-        out_shape=(
-            jax.ShapeDtypeStruct((levels, 1, cells), F32),
-            jax.ShapeDtypeStruct((levels, 1, cells), F32),
-            jax.ShapeDtypeStruct((levels, 1, edges), F32),
-        ),
+        out_shape=tuple(pltpu.VMEM((levels, width), F32) for width in widths),
         in_specs=[hbm] * len(arguments),
-        out_specs=(hbm,) * 3,
+        out_specs=(vmem,) * 3,
         scratch_shapes=[
             *(pltpu.VMEM(x.shape[1:], x.dtype) for x in landed),
-            pltpu.VMEM((levels, cells), F32),
-            pltpu.VMEM((levels, cells), F32),
-            pltpu.VMEM((levels, edges), F32),
             pltpu.VMEM((padded, edges_ext), F32),
             pltpu.VMEM((padded, cells_ext), F32),
             pltpu.VMEM((padded, cells_ext), F32),
@@ -355,10 +350,16 @@
             pltpu.SemaphoreType.DMA((slots,)),
             pltpu.SemaphoreType.DMA((slots,)),
             pltpu.SemaphoreType.DMA((len(arguments),)),
-            pltpu.SemaphoreType.DMA((3,)),
         ],
         compiler_params=pltpu.CompilerParams(collective_id=0, has_side_effects=True),
     )(*operands)
+    results = pl.pallas_call(
+        deliver,
+        out_shape=tuple(jax.ShapeDtypeStruct((levels, 1, width), F32) for width in widths),
+        in_specs=[vmem] * 3,
+        out_specs=(hbm,) * 3,
+        scratch_shapes=[pltpu.SemaphoreType.DMA((3,))],
+    )(*(pltpu.with_memory_space_constraint(x, pltpu.VMEM) for x in results))
     return tuple(jnp.transpose(x, (1, 0, 2)) for x in results)
 
 

time: 22.3 us -> 18.5 us (0.83)
  local copies, waits for them, and re-layouts: 3.6 us -> 0 us
    unnamed x5 -> x0, local copies, waits for them, and re-layouts: 3.6 us -> none
    pallas_call x1 -> x2, Pallas kernels: 17.8 us -> 17.7 us  [the longest x1 16.9 us: shards(): pl.pallas_call(kernel, out_shape=tuple((pltpu.VMEM((levels, width), F32)...]
where the time goes in v1:
time: 18.5 us; the launch traced here: 18.3 us
  Pallas kernels  17.7 us (96%)
  between operations  0.64 us (3%)
    pallas_call x1, Pallas kernels, shards(): pl.pallas_call(kernel, out_shape=tuple((pltpu.VMEM((levels, width), F32)...  16.9 us
    pallas_call x1, Pallas kernels, shards(): pl.pallas_call(deliver, out_shape=tuple((jax.ShapeDtypeStruct((levels, 1,...  0.73 us

profile of v1, /device:TPU:0, one launch (start us, length us, event | category | flops | bytes accessed | tf_op | source)
XLA Modules:
  0.0 18.3 jit_solution(2275730276868284772)
XLA Ops:
  0.6 16.9 %shard_map.130 = (f32[55,256]{1,0:T(8,128)S(1)}, f32[55,256]{1,0:T(8,128)S(1)}, f32[55,768]{1,0:T(8,128)S(1)}) custom-call(f32[55,1,768]{2,1,0:T(1,128)} %bitcast.13, f32[55,1,256]{2,1,0:T(1,128)} %bitcast.14, f32[55,1,256]{2,1,0:T(1,128)} %bitcast.15, s32[6,1,256]{2,1,0:T(1,128)} %bitcast.19, s32[1,2,1664]{2,1,0:T(2,128)} %edge_cells_hbm.1, ...), custom_call_target="tpu_custom_call" | custom-call | tf_op jit(solution)/shard_map/pallas_call | solution.py:323
  17.6 0.7 %shard_map.131 = (f32[55,1,256]{2,1,0:T(1,128)}, f32[55,1,256]{2,1,0:T(1,128)}, f32[55,1,768]{2,1,0:T(1,128)}) custom-call(f32[55,256]{1,0:T(8,128)S(1)} %get-tuple-element.9.refs_0_, f32[55,256]{1,0:T(8,128)S(1)} %get-tuple-element.10.refs_1_, f32[55,768]{1,0:T(8,128)S(1)} %get-tuple-element.11.refs_2_), custom_call_target="tpu_custom_call" | custom-call | tf_op jit(solution)/shard_map/pallas_call | solution.py:356

commit v2 on v1

--- a/solution.py
+++ b/solution.py
@@ -10,6 +10,14 @@
 STEP_SIZE = 0.2
 OFFSETS = (1, -1, 2, -2, 3, -3)
 SEND_ORDER = (4, 5, 2, 3, 0, 1, 6)
+WRAP_ORDERS = {
+    -1: (0, 2, 4, 5, 3, 1, 6),
+    -2: (2, 4, 5, 3, 0, 1, 6),
+    0: (1, 3, 5, 4, 2, 0, 6),
+    1: (3, 5, 4, 2, 0, 1, 6),
+    2: (5, 4, 3, 2, 0, 1, 6),
+}
+URGENT = 3
 LANES = 128
 F32 = jnp.float32
 BF16 = jnp.bfloat16
@@ -33,7 +41,14 @@
     return total
 
 
-def build(index_ref, weight_ref, lead_ref, trail_ref):
+def moved(indices, owned, halo, shifts):
+    shift = jnp.zeros_like(indices)
+    for slot, amount in enumerate(shifts):
+        shift = jnp.where(indices >= owned + slot * halo, amount * halo, shift)
+    return indices + shift
+
+
+def build(index_ref, weight_ref, lead_ref, trail_ref, first=0, last=None):
     terms = weight_ref.shape[0]
     row_tiles = lead_ref.shape[0] // LANES
     column_tiles = lead_ref.shape[1] // LANES
@@ -56,7 +71,7 @@
             trail_ref[pl.ds(row, LANES), columns] = (matrix - lead.astype(F32)).astype(BF16)
         return carry
 
-    lax.fori_loop(0, row_tiles * column_tiles, tile, 0)
+    lax.fori_loop(first, row_tiles * column_tiles if last is None else last, tile, 0)
 
 
 def spread(indices, weights, index_ref, lead_ref, trail_ref):
@@ -128,9 +143,20 @@
     padded = wind_ext.shape[0]
 
     def target(slot):
-        if slot < len(OFFSETS):
+        if isinstance(slot, int):
+            if slot == len(OFFSETS):
+                return (position, 1 - side)
             return (lax.rem(position + OFFSETS[slot] + blocks, blocks), side)
-        return (position, 1 - side)
+        offset = (lax.div(slot, 2) + 1) * (1 - 2 * lax.rem(slot, 2))
+        across = slot == len(OFFSETS)
+        offset = jnp.where(across, 0, offset)
+        return (lax.rem(position + offset + blocks, blocks), jnp.where(across, 1 - side, side))
+
+    barrier = pltpu.get_barrier_semaphore()
+    for slot in SEND_ORDER:
+        pl.semaphore_signal(
+            barrier, inc=1, device_id=target(slot), device_id_type=pl.DeviceIdType.MESH
+        )
 
     loads = (
         (send_edges_hbm, send_edges_ref),
@@ -154,12 +180,6 @@
     for load in loads:
         load.start()
 
-    barrier = pltpu.get_barrier_semaphore()
-    for slot in range(slots):
-        pl.semaphore_signal(
-            barrier, inc=1, device_id=target(slot), device_id_type=pl.DeviceIdType.MESH
-        )
-
     for load in loads[:5]:
         load.wait()
     for ext, ref in ((wind_ext, wind_ref), (density_ext, density_ref), (theta_ext, theta_ref)):
@@ -172,22 +192,37 @@
         if spare < ext.shape[1]:
             ext[:, spare:] = jnp.zeros((padded, ext.shape[1] - spare), F32)
 
-    wind_own = halves(wind_ext[:, 0:edges])
-    cells_own = halves(
-        jnp.concatenate([density_ext[:, 0:cells], theta_ext[:, 0:cells]], axis=0)
-    )
+    upper = 2 * position >= blocks
+    parity = jnp.where(upper, 1, 0)
+    rank = [
+        jnp.where(parity == slot % 2, 4 + slot // 2, 1 + slot // 2) for slot in range(len(OFFSETS))
+    ] + [0]
+    shifts = [rank[slot] - slot for slot in range(slots)]
+
+    order = []
+    for step, slot in enumerate(SEND_ORDER):
+        for place, slots_there in WRAP_ORDERS.items():
+            slot = jnp.where(position == lax.rem(place + blocks, blocks), slots_there[step], slot)
+        order.append(slot)
 
     edge_rows = lax.broadcasted_iota(jnp.int32, (edges, halo_edges), 0)
     cell_rows = lax.broadcasted_iota(jnp.int32, (cells, halo_cells), 0)
-    for slot in range(slots):
-        picks = jnp.where(edge_rows == send_edges_ref[slot : slot + 1, :], 1.0, 0.0).astype(BF16)
-        both = dot(wind_own, picks)
-        send[slot, :, 2 * halo_cells :] = both[0:padded] + both[padded:]
-        picks = jnp.where(cell_rows == send_cells_ref[slot : slot + 1, :], 1.0, 0.0).astype(BF16)
-        both = dot(cells_own, picks)
-        both = both[0 : 2 * padded] + both[2 * padded :]
-        send[slot, :, 0:halo_cells] = both[0:padded]
-        send[slot, :, halo_cells : 2 * halo_cells] = both[padded:]
+
+    def gather(some):
+        wind_own = halves(wind_ext[:, 0:edges])
+        cells_own = halves(
+            jnp.concatenate([density_ext[:, 0:cells], theta_ext[:, 0:cells]], axis=0)
+        )
+        for slot in some:
+            row = pl.ds(slot, 1)
+            picks = jnp.where(edge_rows == send_edges_ref[row, :], 1.0, 0.0).astype(BF16)
+            both = dot(wind_own, picks)
+            send[slot, :, 2 * halo_cells :] = both[0:padded] + both[padded:]
+            picks = jnp.where(cell_rows == send_cells_ref[row, :], 1.0, 0.0).astype(BF16)
+            both = dot(cells_own, picks)
+            both = both[0 : 2 * padded] + both[2 * padded :]
+            send[slot, :, 0:halo_cells] = both[0:padded]
+            send[slot, :, halo_cells : 2 * halo_cells] = both[padded:]
 
     def copy_of(slot):
         return pltpu.make_async_remote_copy(
@@ -199,24 +234,64 @@
             device_id_type=pl.DeviceIdType.MESH,
         )
 
-    pl.semaphore_wait(barrier, slots)
-    for slot in SEND_ORDER:
-        copy_of(slot).start()
-
+    def prepare_tangent():
+        indices = moved(edges_on_edge_ref[...], edges, halo_edges, shifts)
+        tangent_weight[...] = merged_weights(indices, eoe_weight_ref[...])
+        edges_on_edge_ref[...] = indices
+
+    tangent_steps = (tangent.shape[0] // LANES) * (tangent.shape[1] // LANES)
+    tangent_ahead = jnp.where(
+        position == 0, 5 * tangent_steps // 6, jnp.where(position < 3, tangent_steps // 2, 0)
+    )
+    early = position < 3
+
+    gather(order[:URGENT])
     for load in loads[5:]:
         load.wait()
-    tangent_weight[...] = merged_weights(edges_on_edge_ref[...], eoe_weight_ref[...])
-    diverge_weight[...] = merged_weights(cell_edges_ref[...], cell_weight_ref[...])
+
+    @pl.when(early)
+    def _():
+        gather(order[URGENT:])
+        prepare_tangent()
+        build(edges_on_edge_ref, tangent_weight, tangent, tangent_trail, 0, tangent_ahead)
+
+    pl.semaphore_wait(barrier, slots)
+    for slot in order[:URGENT]:
+        copy_of(slot).start()
+
+    @pl.when(jnp.logical_not(early))
+    def _():
+        gather(order[URGENT:])
+
+    for slot in order[URGENT:]:
+        copy_of(slot).start()
+
+    @pl.when(jnp.logical_not(early))
+    def _():
+        prepare_tangent()
+
+    indices = moved(cell_edges_ref[...], edges, halo_edges, shifts)
+    diverge_weight[...] = merged_weights(indices, cell_weight_ref[...])
+    cell_edges_ref[...] = indices
     average_tables = (average_index, average_lead, None)
+    indices = moved(edge_cells_ref[...], cells, halo_cells, shifts)
+    edge_cells_ref[:, 0:edges] = indices[:, 0:edges]
+    for slot in range(slots):
+        start = edges + slot * halo_edges
+        place = pl.multiple_of(edges + rank[slot] * halo_edges, LANES)
+        edge_cells_ref[:, pl.ds(place, halo_edges)] = indices[:, start : start + halo_edges]
+    indices = edge_cells_ref[...]
     spread(
-        edge_cells_ref[...],
-        merged_weights(edge_cells_ref[...], jnp.full(edge_cells_ref.shape, 0.5, F32)),
+        indices,
+        merged_weights(indices, jnp.full(edge_cells_ref.shape, 0.5, F32)),
         *average_tables,
     )
     places[...] = lax.broadcasted_iota(jnp.int32, places.shape, 0).astype(jnp.int16)
     build_packed(average.shape[0], places, average_tables, average, None)
     build(cell_edges_ref, diverge_weight, diverge, diverge_trail)
-    build(edges_on_edge_ref, tangent_weight, tangent, tangent_trail)
+    build(
+        edges_on_edge_ref, tangent_weight, tangent, tangent_trail, tangent_ahead, tangent_steps
+    )
 
     ratio = jnp.zeros((1, cells), F32)
     below = jnp.zeros((1, cells), F32)
@@ -232,33 +307,43 @@
         ratios[level : level + 1, :] = ratio
         below = above
 
-    wind_own = halves(wind_ext[:, 0:edges])
-    both = dot(wind_own, tangent[0:edges, :])
-    tangent_sum[...] = both[0:padded] + both[padded:] + dot(
-        wind_own[0:padded], tangent_trail[0:edges, :]
-    )
-    own = density_ext[:, 0:cells]
-    both = dot(
-        halves(jnp.concatenate([own, own * theta_ext[:, 0:cells]], axis=0)),
-        average[0:cells, :],
-    )
-    average_sum[...] = both[0 : 2 * padded] + both[2 * padded :]
-
-    for slot in SEND_ORDER:
+    def tangent_part(lower, higher):
+        part = halves(wind_ext[:, lower:higher])
+        both = dot(part, tangent[lower:higher, :])
+        return both[0:padded] + both[padded:] + dot(
+            part[0:padded], tangent_trail[lower:higher, :]
+        )
+
+    def average_part(lower, higher):
+        part = density_ext[:, lower:higher]
+        both = dot(
+            halves(jnp.concatenate([part, part * theta_ext[:, lower:higher]], axis=0)),
+            average[lower:higher, :],
+        )
+        return both[0 : 2 * padded] + both[2 * padded :]
+
+    def take(slot, place):
         copy_of(slot).wait_recv()
-    for slot in range(slots):
-        start = cells + slot * halo_cells
+        start = cells + place * halo_cells
         density_ext[:, start : start + halo_cells] = received[slot, :, 0:halo_cells]
         theta_ext[:, start : start + halo_cells] = received[slot, :, halo_cells : 2 * halo_cells]
-        start = edges + slot * halo_edges
+        start = edges + place * halo_edges
         wind_ext[:, start : start + halo_edges] = received[slot, :, 2 * halo_cells :]
 
-    halo = density_ext[:, cells:]
-    both = dot(
-        halves(jnp.concatenate([halo, halo * theta_ext[:, cells:]], axis=0)),
-        average[cells:, :],
-    )
-    averaged = average_sum[...] + both[0 : 2 * padded] + both[2 * padded :]
+    tangent_sum[...] = tangent_part(0, edges)
+    average_sum[...] = average_part(0, cells)
+
+    near = 1 + len(OFFSETS) // 2
+    take(slots - 1, 0)
+    for pair in range(near - 1):
+        take(2 * pair + 1 - parity, 1 + pair)
+    edges_near, cells_near = edges + near * halo_edges, cells + near * halo_cells
+    tangent_sum[...] += tangent_part(edges, edges_near)
+    average_sum[...] += average_part(cells, cells_near)
+
+    for pair in range(near - 1):
+        take(2 * pair + parity, near + pair)
+    averaged = average_sum[...] + average_part(cells_near, density_ext.shape[1])
     wind = wind_ext[...]
     fluxes = halves(jnp.concatenate([wind, wind], axis=0) * averaged)
     both = dot(fluxes, diverge[...])
@@ -269,11 +354,7 @@
     values[...] = (theta_ext[:, 0:cells] - STEP_SIZE * divergence[padded:])
     values[0:levels, :] = values[0:levels, :] * inverse[0:levels, :]
 
-    wind_halo = halves(wind_ext[:, edges:])
-    both = dot(wind_halo, tangent[edges:, :])
-    tangential = tangent_sum[...] + both[0:padded] + both[padded:] + dot(
-        wind_halo[0:padded], tangent_trail[edges:, :]
-    )
+    tangential = tangent_sum[...] + tangent_part(edges_near, wind_ext.shape[1])
     tangential_ref[...] = tangential[0:levels]
 
     value = jnp.zeros((1, cells), F32)

time: 18.5 us -> 16 us (0.86)
  Pallas kernels: 17.7 us -> 15.2 us
    pallas_call x1, Pallas kernels: 16.9 us -> 14.4 us  [shards(): pl.pallas_call(kernel, out_shape=tuple((pltpu.VMEM((levels, width), F32)...]
where the time goes in v2:
time: 16 us; the launch traced here: 15.8 us
  Pallas kernels  15.2 us (95%)
  between operations  0.64 us (4%)
    pallas_call x1, Pallas kernels, shards(): pl.pallas_call(kernel, out_shape=tuple((pltpu.VMEM((levels, width), F32)...  14.4 us
    pallas_call x1, Pallas kernels, shards(): pl.pallas_call(deliver, out_shape=tuple((jax.ShapeDtypeStruct((levels, 1,...  0.73 us

profile of v2, /device:TPU:0, one launch (start us, length us, event | category | flops | bytes accessed | tf_op | source)
XLA Modules:
  0.0 15.8 jit_solution(10336278216636407001)
XLA Ops:
  0.6 14.4 %shard_map.130 = (f32[55,256]{1,0:T(8,128)S(1)}, f32[55,256]{1,0:T(8,128)S(1)}, f32[55,768]{1,0:T(8,128)S(1)}) custom-call(f32[55,1,768]{2,1,0:T(1,128)} %bitcast.13, f32[55,1,256]{2,1,0:T(1,128)} %bitcast.14, f32[55,1,256]{2,1,0:T(1,128)} %bitcast.15, s32[6,1,256]{2,1,0:T(1,128)} %bitcast.19, s32[1,2,1664]{2,1,0:T(2,128)} %edge_cells_hbm.1, ...), custom_call_target="tpu_custom_call" | custom-call | tf_op jit(solution)/shard_map/pallas_call | solution.py:404
  15.1 0.7 %shard_map.131 = (f32[55,1,256]{2,1,0:T(1,128)}, f32[55,1,256]{2,1,0:T(1,128)}, f32[55,1,768]{2,1,0:T(1,128)}) custom-call(f32[55,256]{1,0:T(8,128)S(1)} %get-tuple-element.9.refs_0_, f32[55,256]{1,0:T(8,128)S(1)} %get-tuple-element.10.refs_1_, f32[55,768]{1,0:T(8,128)S(1)} %get-tuple-element.11.refs_2_), custom_call_target="tpu_custom_call" | custom-call | tf_op jit(solution)/shard_map/pallas_call | solution.py:437

commit v3 on v2

--- a/solution.py
+++ b/solution.py
@@ -19,6 +19,7 @@
 }
 URGENT = 3
 LANES = 128
+PACKED = 16
 F32 = jnp.float32
 BF16 = jnp.bfloat16
 
@@ -48,76 +49,43 @@
     return indices + shift
 
 
-def build(index_ref, weight_ref, lead_ref, trail_ref, first=0, last=None):
+def build(index_ref, weight_ref, lead_ref, trail_ref, chunk, first=0, last=None):
     terms = weight_ref.shape[0]
-    row_tiles = lead_ref.shape[0] // LANES
+    row_tiles = lead_ref.shape[0] // chunk
     column_tiles = lead_ref.shape[1] // LANES
-
-    def tile(step, carry):
-        row = pl.multiple_of(lax.rem(step, row_tiles) * LANES, LANES)
-        column = pl.multiple_of(lax.div(step, row_tiles) * LANES, LANES)
-        columns = pl.ds(column, LANES)
-        positions = lax.broadcasted_iota(jnp.int32, (LANES, LANES), 0) + row
-        matrix = jnp.zeros((LANES, LANES), F32)
-        for term in range(terms):
-            matrix = jnp.where(
-                positions == index_ref[term : term + 1, columns],
-                weight_ref[term : term + 1, columns],
-                matrix,
-            )
-        lead = matrix.astype(BF16)
-        lead_ref[pl.ds(row, LANES), columns] = lead
-        if trail_ref is not None:
-            trail_ref[pl.ds(row, LANES), columns] = (matrix - lead.astype(F32)).astype(BF16)
-        return carry
-
-    lax.fori_loop(first, row_tiles * column_tiles if last is None else last, tile, 0)
-
-
-def spread(indices, weights, index_ref, lead_ref, trail_ref):
-    terms, outputs = indices.shape
-    rows = index_ref.shape[1]
-    lead = weights.astype(BF16).astype(F32)
-    for term in range(terms):
-        def tiled(table):
-            return jnp.broadcast_to(table[term : term + 1], (rows, outputs))
-
-        index_ref[term] = tiled(indices).astype(jnp.int16)
-        lead_ref[term] = tiled(lead).astype(BF16)
-        if trail_ref is not None:
-            trail_ref[term] = tiled(weights - lead).astype(BF16)
-
-
-def build_packed(chunk, place_ref, tables, lead_out, trail_out):
-    index_ref, lead_ref, trail_ref = tables
-    terms, rows = index_ref.shape[:2]
-    row_tiles = lead_out.shape[0] // chunk
-    column_tiles = lead_out.shape[1] // LANES
+    base = lax.broadcasted_iota(jnp.int32, (PACKED, LANES), 0).astype(jnp.int16)
+    zero = jnp.zeros((PACKED, LANES), F32).astype(BF16)
 
     def tile(step, carry):
         row = pl.multiple_of(lax.rem(step, row_tiles) * chunk, chunk)
         column = pl.multiple_of(lax.div(step, row_tiles) * LANES, LANES)
         columns = pl.ds(column, LANES)
-        zero = jnp.zeros((rows, LANES), BF16)
-        indices = [index_ref[term, :, columns] for term in range(terms)]
-        leads = [lead_ref[term, :, columns] for term in range(terms)]
-        if trail_out is not None:
-            trails = [trail_ref[term, :, columns] for term in range(terms)]
-        for part in range(chunk // rows):
-            here = pl.ds(row + part * rows, rows)
-            places = place_ref[here, :]
+
+        def rows_of(ref, term):
+            return jnp.broadcast_to(ref[term : term + 1, columns], (PACKED, LANES))
+
+        indices = [(rows_of(index_ref, term) - row).astype(jnp.int16) for term in range(terms)]
+        weights = [rows_of(weight_ref, term) for term in range(terms)]
+        leads = [weight.astype(BF16) for weight in weights]
+        if trail_ref is not None:
+            trails = [
+                (weight - lead.astype(F32)).astype(BF16) for weight, lead in zip(weights, leads)
+            ]
+        for part in range(chunk // PACKED):
+            here = pl.ds(row + part * PACKED, PACKED)
+            places = base + jnp.int16(part * PACKED)
             lead, trail = zero, zero
             for term in range(terms):
                 hit = places == indices[term]
                 lead = jnp.where(hit, leads[term], lead)
-                if trail_out is not None:
+                if trail_ref is not None:
                     trail = jnp.where(hit, trails[term], trail)
-            lead_out[here, columns] = lead
-            if trail_out is not None:
-                trail_out[here, columns] = trail
+            lead_ref[here, columns] = lead
+            if trail_ref is not None:
+                trail_ref[here, columns] = trail
         return carry
 
-    lax.fori_loop(0, row_tiles * column_tiles, tile, 0)
+    lax.fori_loop(first, row_tiles * column_tiles if last is None else last, tile, 0)
 
 
 def kernel(
@@ -128,7 +96,7 @@
     cell_edges_ref, edge_cells_ref, edges_on_edge_ref, send_cells_ref, send_edges_ref,
     cell_weight_ref, eoe_weight_ref, coupling_ref,
     wind_ext, density_ext, theta_ext, send, received,
-    average, average_index, average_lead, places, diverge, diverge_trail, diverge_weight,
+    average, average_weight, diverge, diverge_trail, diverge_weight,
     tangent, tangent_trail, tangent_weight,
     average_sum, tangent_sum, inverse, carried, ratios, values,
     send_sem, recv_sem, load_sem,
@@ -239,7 +207,8 @@
         tangent_weight[...] = merged_weights(indices, eoe_weight_ref[...])
         edges_on_edge_ref[...] = indices
 
-    tangent_steps = (tangent.shape[0] // LANES) * (tangent.shape[1] // LANES)
+    chunk = tangent.shape[0] // 2
+    tangent_steps = 2 * (tangent.shape[1] // LANES)
     tangent_ahead = jnp.where(
         position == 0, 5 * tangent_steps // 6, jnp.where(position < 3, tangent_steps // 2, 0)
     )
@@ -253,7 +222,7 @@
     def _():
         gather(order[URGENT:])
         prepare_tangent()
-        build(edges_on_edge_ref, tangent_weight, tangent, tangent_trail, 0, tangent_ahead)
+        build(edges_on_edge_ref, tangent_weight, tangent, tangent_trail, chunk, 0, tangent_ahead)
 
     pl.semaphore_wait(barrier, slots)
     for slot in order[:URGENT]:
@@ -273,24 +242,19 @@
     indices = moved(cell_edges_ref[...], edges, halo_edges, shifts)
     diverge_weight[...] = merged_weights(indices, cell_weight_ref[...])
     cell_edges_ref[...] = indices
-    average_tables = (average_index, average_lead, None)
     indices = moved(edge_cells_ref[...], cells, halo_cells, shifts)
     edge_cells_ref[:, 0:edges] = indices[:, 0:edges]
     for slot in range(slots):
         start = edges + slot * halo_edges
         place = pl.multiple_of(edges + rank[slot] * halo_edges, LANES)
         edge_cells_ref[:, pl.ds(place, halo_edges)] = indices[:, start : start + halo_edges]
-    indices = edge_cells_ref[...]
-    spread(
-        indices,
-        merged_weights(indices, jnp.full(edge_cells_ref.shape, 0.5, F32)),
-        *average_tables,
-    )
-    places[...] = lax.broadcasted_iota(jnp.int32, places.shape, 0).astype(jnp.int16)
-    build_packed(average.shape[0], places, average_tables, average, None)
-    build(cell_edges_ref, diverge_weight, diverge, diverge_trail)
+    average_weight[...] = merged_weights(
+        edge_cells_ref[...], jnp.full(edge_cells_ref.shape, 0.5, F32)
+    )
+    build(edge_cells_ref, average_weight, average, None, average.shape[0])
+    build(cell_edges_ref, diverge_weight, diverge, diverge_trail, chunk)
     build(
-        edges_on_edge_ref, tangent_weight, tangent, tangent_trail, tangent_ahead, tangent_steps
+        edges_on_edge_ref, tangent_weight, tangent, tangent_trail, chunk, tangent_ahead, tangent_steps
     )
 
     ratio = jnp.zeros((1, cells), F32)
@@ -380,11 +344,6 @@
         store.start()
     for store in stores:
         store.wait()
-
-
-def spread_of(table):
-    shape = (table.shape[1], 16, table.shape[2])
-    return [pltpu.VMEM(shape, kind) for kind in (jnp.int16, BF16, BF16)]
 
 
 def shards(*arguments):
@@ -414,8 +373,7 @@
             pltpu.VMEM((slots, padded, 2 * halo_cells + halo_edges), F32),
             pltpu.VMEM((slots, padded, 2 * halo_cells + halo_edges), F32),
             pltpu.VMEM((cells_ext, edges_ext), BF16),
-            *spread_of(edge_cells)[:2],
-            pltpu.VMEM((cells_ext, LANES), jnp.int16),
+            pltpu.VMEM(edge_cells.shape[1:], F32),
             pltpu.VMEM((edges_ext, cells), BF16),
             pltpu.VMEM((edges_ext, cells), BF16),
             pltpu.VMEM(cell_edges.shape[1:], F32),

time: 16 us -> 15.7 us (0.981)
  Pallas kernels: 15.2 us -> 14.9 us
    pallas_call x1, Pallas kernels: 14.4 us -> 14.2 us  [shards(): pl.pallas_call(kernel, out_shape=tuple((pltpu.VMEM((levels, width), F32)...]
where the time goes in v3:
time: 15.7 us; the launch traced here: 15.5 us
  Pallas kernels  14.9 us (95%)
  between operations  0.64 us (4%)
    pallas_call x1, Pallas kernels, shards(): pl.pallas_call(kernel, out_shape=tuple((pltpu.VMEM((levels, width), F32)...  14.2 us
    pallas_call x1, Pallas kernels, shards(): pl.pallas_call(deliver, out_shape=tuple((jax.ShapeDtypeStruct((levels, 1,...  0.73 us

profile of v3, /device:TPU:0, one launch (start us, length us, event | category | flops | bytes accessed | tf_op | source)
XLA Modules:
  0.0 15.5 jit_solution(3547007949489578883)
XLA Ops:
  0.6 14.2 %shard_map.130 = (f32[55,256]{1,0:T(8,128)S(1)}, f32[55,256]{1,0:T(8,128)S(1)}, f32[55,768]{1,0:T(8,128)S(1)}) custom-call(f32[55,1,768]{2,1,0:T(1,128)} %bitcast.13, f32[55,1,256]{2,1,0:T(1,128)} %bitcast.14, f32[55,1,256]{2,1,0:T(1,128)} %bitcast.15, s32[6,1,256]{2,1,0:T(1,128)} %bitcast.19, s32[1,2,1664]{2,1,0:T(2,128)} %edge_cells_hbm.1, ...), custom_call_target="tpu_custom_call" | custom-call | tf_op jit(solution)/shard_map/pallas_call | solution.py:363
  14.8 0.7 %shard_map.131 = (f32[55,1,256]{2,1,0:T(1,128)}, f32[55,1,256]{2,1,0:T(1,128)}, f32[55,1,768]{2,1,0:T(1,128)}) custom-call(f32[55,256]{1,0:T(8,128)S(1)} %get-tuple-element.9.refs_0_, f32[55,256]{1,0:T(8,128)S(1)} %get-tuple-element.10.refs_1_, f32[55,768]{1,0:T(8,128)S(1)} %get-tuple-element.11.refs_2_), custom_call_target="tpu_custom_call" | custom-call | tf_op jit(solution)/shard_map/pallas_call | solution.py:395

commit v4 on v3

--- a/solution.py
+++ b/solution.py
@@ -13,9 +13,9 @@
 WRAP_ORDERS = {
     -1: (0, 2, 4, 5, 3, 1, 6),
     -2: (2, 4, 5, 3, 0, 1, 6),
-    0: (1, 3, 5, 4, 2, 0, 6),
-    1: (3, 5, 4, 2, 0, 1, 6),
-    2: (5, 4, 3, 2, 0, 1, 6),
+    0: (4, 2, 0, 6, 1, 3, 5),
+    1: (1, 4, 2, 0, 6, 3, 5),
+    2: (3, 1, 4, 2, 0, 6, 5),
 }
 URGENT = 3
 LANES = 128
@@ -99,7 +99,7 @@
     average, average_weight, diverge, diverge_trail, diverge_weight,
     tangent, tangent_trail, tangent_weight,
     average_sum, tangent_sum, inverse, carried, ratios, values,
-    send_sem, recv_sem, load_sem,
+    send_sem, recv_sem, load_sem, near_sem, far_sem,
 ):
     blocks = lax.axis_size("blk")
     position = lax.axis_index("blk")
@@ -121,10 +121,24 @@
         return (lax.rem(position + offset + blocks, blocks), jnp.where(across, 1 - side, side))
 
     barrier = pltpu.get_barrier_semaphore()
+    reach = len(OFFSETS) // 2
+    first = position == 0
+    waits_far = jnp.where(first, 0, jnp.maximum(reach - position, 0))
+    late = jnp.where(first, reach + 1, waits_far)
+
+    def signal(semaphore, slot):
+        pl.semaphore_signal(
+            semaphore, inc=1, device_id=target(slot), device_id_type=pl.DeviceIdType.MESH
+        )
+
+    def later(slot):
+        if slot == len(OFFSETS):
+            return first & (side == 1)
+        there = position + OFFSETS[slot]
+        return there > blocks if OFFSETS[slot] > 0 else there == 0
+
     for slot in SEND_ORDER:
-        pl.semaphore_signal(
-            barrier, inc=1, device_id=target(slot), device_id_type=pl.DeviceIdType.MESH
-        )
+        pl.when(jnp.logical_not(later(slot)))(functools.partial(signal, barrier, slot))
 
     loads = (
         (send_edges_hbm, send_edges_ref),
@@ -202,60 +216,74 @@
             device_id_type=pl.DeviceIdType.MESH,
         )
 
-    def prepare_tangent():
+    chunk = tangent.shape[0] // 2
+    steps = 2 * (tangent.shape[1] // LANES)
+    steps_ahead = jnp.where(first, jnp.where(side == 0, 3 * steps // 4, steps // 2), 0)
+
+    def prepare():
         indices = moved(edges_on_edge_ref[...], edges, halo_edges, shifts)
         tangent_weight[...] = merged_weights(indices, eoe_weight_ref[...])
         edges_on_edge_ref[...] = indices
-
-    chunk = tangent.shape[0] // 2
-    tangent_steps = 2 * (tangent.shape[1] // LANES)
-    tangent_ahead = jnp.where(
-        position == 0, 5 * tangent_steps // 6, jnp.where(position < 3, tangent_steps // 2, 0)
-    )
-    early = position < 3
+        indices = moved(cell_edges_ref[...], edges, halo_edges, shifts)
+        diverge_weight[...] = merged_weights(indices, cell_weight_ref[...])
+        cell_edges_ref[...] = indices
+        indices = moved(edge_cells_ref[...], cells, halo_cells, shifts)
+        edge_cells_ref[:, 0:edges] = indices[:, 0:edges]
+        for slot in range(slots):
+            start = edges + slot * halo_edges
+            place = pl.multiple_of(edges + rank[slot] * halo_edges, LANES)
+            edge_cells_ref[:, pl.ds(place, halo_edges)] = indices[:, start : start + halo_edges]
+        average_weight[...] = merged_weights(
+            edge_cells_ref[...], jnp.full(edge_cells_ref.shape, 0.5, F32)
+        )
+        build(edge_cells_ref, average_weight, average, None, average.shape[0])
+        build(cell_edges_ref, diverge_weight, diverge, diverge_trail, chunk)
+
+    def build_tangent(lower, higher):
+        build(edges_on_edge_ref, tangent_weight, tangent, tangent_trail, chunk, lower, higher)
 
     gather(order[:URGENT])
     for load in loads[5:]:
         load.wait()
 
-    @pl.when(early)
+    @pl.when(first)
     def _():
-        gather(order[URGENT:])
-        prepare_tangent()
-        build(edges_on_edge_ref, tangent_weight, tangent, tangent_trail, chunk, 0, tangent_ahead)
-
-    pl.semaphore_wait(barrier, slots)
+        prepare()
+        build_tangent(0, steps_ahead)
+
+    @pl.when(first)
+    def _():
+        pl.semaphore_wait(near_sem, reach)
+
+    @pl.when(jnp.logical_not(first))
+    def _():
+        pl.semaphore_wait(barrier, slots - waits_far)
+        for slot, offset in enumerate(OFFSETS):
+            greeted = far_sem if offset > 0 else near_sem
+            pl.when(later(slot))(functools.partial(signal, greeted, slot))
+
     for slot in order[:URGENT]:
         copy_of(slot).start()
-
-    @pl.when(jnp.logical_not(early))
+    gather(order[URGENT:])
+    for step, slot in enumerate(order[URGENT:], URGENT):
+        pl.when(step < slots - late)(copy_of(slot).start)
+
+    pl.when(jnp.logical_not(first))(prepare)
+    build_tangent(steps_ahead, steps)
+
+    @pl.when(first)
     def _():
-        gather(order[URGENT:])
-
-    for slot in order[URGENT:]:
-        copy_of(slot).start()
-
-    @pl.when(jnp.logical_not(early))
+        pl.semaphore_wait(barrier, reach + side)
+        pl.when(side == 1)(functools.partial(signal, far_sem, slots - 1))
+
+    greetings = jnp.where(first, 1 - side, waits_far)
+
+    @pl.when(greetings > 0)
     def _():
-        prepare_tangent()
-
-    indices = moved(cell_edges_ref[...], edges, halo_edges, shifts)
-    diverge_weight[...] = merged_weights(indices, cell_weight_ref[...])
-    cell_edges_ref[...] = indices
-    indices = moved(edge_cells_ref[...], cells, halo_cells, shifts)
-    edge_cells_ref[:, 0:edges] = indices[:, 0:edges]
-    for slot in range(slots):
-        start = edges + slot * halo_edges
-        place = pl.multiple_of(edges + rank[slot] * halo_edges, LANES)
-        edge_cells_ref[:, pl.ds(place, halo_edges)] = indices[:, start : start + halo_edges]
-    average_weight[...] = merged_weights(
-        edge_cells_ref[...], jnp.full(edge_cells_ref.shape, 0.5, F32)
-    )
-    build(edge_cells_ref, average_weight, average, None, average.shape[0])
-    build(cell_edges_ref, diverge_weight, diverge, diverge_trail, chunk)
-    build(
-        edges_on_edge_ref, tangent_weight, tangent, tangent_trail, chunk, tangent_ahead, tangent_steps
-    )
+        pl.semaphore_wait(far_sem, greetings)
+
+    for step, slot in enumerate(order[URGENT:], URGENT):
+        pl.when(step >= slots - late)(copy_of(slot).start)
 
     ratio = jnp.zeros((1, cells), F32)
     below = jnp.zeros((1, cells), F32)
@@ -297,7 +325,7 @@
     tangent_sum[...] = tangent_part(0, edges)
     average_sum[...] = average_part(0, cells)
 
-    near = 1 + len(OFFSETS) // 2
+    near = 1 + reach
     take(slots - 1, 0)
     for pair in range(near - 1):
         take(2 * pair + 1 - parity, 1 + pair)
@@ -389,6 +417,8 @@
             pltpu.SemaphoreType.DMA((slots,)),
             pltpu.SemaphoreType.DMA((slots,)),
             pltpu.SemaphoreType.DMA((len(arguments),)),
+            pltpu.SemaphoreType.REGULAR,
+            pltpu.SemaphoreType.REGULAR,
         ],
         compiler_params=pltpu.CompilerParams(collective_id=0, has_side_effects=True),
     )(*operands)

time: 15.7 us -> 14.6 us (0.930)
  Pallas kernels: 14.9 us -> 13.8 us
    pallas_call x1, Pallas kernels: 14.2 us -> 13.1 us  [shards(): pl.pallas_call(kernel, out_shape=tuple((pltpu.VMEM((levels, width), F32)...]
where the time goes in v4:
time: 14.6 us; the launch traced here: 14.4 us
  Pallas kernels  13.8 us (95%)
  between operations  0.64 us (4%)
    pallas_call x1, Pallas kernels, shards(): pl.pallas_call(kernel, out_shape=tuple((pltpu.VMEM((levels, width), F32)...  13.1 us
    pallas_call x1, Pallas kernels, shards(): pl.pallas_call(deliver, out_shape=tuple((jax.ShapeDtypeStruct((levels, 1,...  0.73 us

profile of v4, /device:TPU:0, one launch (start us, length us, event | category | flops | bytes accessed | tf_op | source)
XLA Modules:
  0.0 14.4 jit_solution(7028599399617901952)
XLA Ops:
  0.6 13.1 %shard_map.130 = (f32[55,256]{1,0:T(8,128)S(1)}, f32[55,256]{1,0:T(8,128)S(1)}, f32[55,768]{1,0:T(8,128)S(1)}) custom-call(f32[55,1,768]{2,1,0:T(1,128)} %bitcast.13, f32[55,1,256]{2,1,0:T(1,128)} %bitcast.14, f32[55,1,256]{2,1,0:T(1,128)} %bitcast.15, s32[6,1,256]{2,1,0:T(1,128)} %bitcast.19, s32[1,2,1664]{2,1,0:T(2,128)} %edge_cells_hbm.1, ...), custom_call_target="tpu_custom_call" | custom-call | tf_op jit(solution)/shard_map/pallas_call | solution.py:391
  13.7 0.7 %shard_map.131 = (f32[55,1,256]{2,1,0:T(1,128)}, f32[55,1,256]{2,1,0:T(1,128)}, f32[55,1,768]{2,1,0:T(1,128)}) custom-call(f32[55,256]{1,0:T(8,128)S(1)} %get-tuple-element.9.refs_0_, f32[55,256]{1,0:T(8,128)S(1)} %get-tuple-element.10.refs_1_, f32[55,768]{1,0:T(8,128)S(1)} %get-tuple-element.11.refs_2_), custom_call_target="tpu_custom_call" | custom-call | tf_op jit(solution)/shard_map/pallas_call | solution.py:425

commit v5 on v4

--- a/solution.py
+++ b/solution.py
@@ -17,7 +17,6 @@
     1: (1, 4, 2, 0, 6, 3, 5),
     2: (3, 1, 4, 2, 0, 6, 5),
 }
-URGENT = 3
 LANES = 128
 PACKED = 16
 F32 = jnp.float32
@@ -120,26 +119,6 @@
         offset = jnp.where(across, 0, offset)
         return (lax.rem(position + offset + blocks, blocks), jnp.where(across, 1 - side, side))
 
-    barrier = pltpu.get_barrier_semaphore()
-    reach = len(OFFSETS) // 2
-    first = position == 0
-    waits_far = jnp.where(first, 0, jnp.maximum(reach - position, 0))
-    late = jnp.where(first, reach + 1, waits_far)
-
-    def signal(semaphore, slot):
-        pl.semaphore_signal(
-            semaphore, inc=1, device_id=target(slot), device_id_type=pl.DeviceIdType.MESH
-        )
-
-    def later(slot):
-        if slot == len(OFFSETS):
-            return first & (side == 1)
-        there = position + OFFSETS[slot]
-        return there > blocks if OFFSETS[slot] > 0 else there == 0
-
-    for slot in SEND_ORDER:
-        pl.when(jnp.logical_not(later(slot)))(functools.partial(signal, barrier, slot))
-
     loads = (
         (send_edges_hbm, send_edges_ref),
         (wind_hbm, wind_ref),
@@ -162,6 +141,26 @@
     for load in loads:
         load.start()
 
+    barrier = pltpu.get_barrier_semaphore()
+    reach = len(OFFSETS) // 2
+    first = position == 0
+    waits_far = jnp.where(first, 0, jnp.maximum(reach - position, 0))
+    late = jnp.where(first, reach + 1, waits_far)
+
+    def signal(semaphore, slot):
+        pl.semaphore_signal(
+            semaphore, inc=1, device_id=target(slot), device_id_type=pl.DeviceIdType.MESH
+        )
+
+    def later(slot):
+        if slot == len(OFFSETS):
+            return first & (side == 1)
+        there = position + OFFSETS[slot]
+        return there > blocks if OFFSETS[slot] > 0 else there == 0
+
+    for slot in SEND_ORDER:
+        pl.when(jnp.logical_not(later(slot)))(functools.partial(signal, barrier, slot))
+
     for load in loads[:5]:
         load.wait()
     for ext, ref in ((wind_ext, wind_ref), (density_ext, density_ref), (theta_ext, theta_ref)):
@@ -174,10 +173,17 @@
         if spare < ext.shape[1]:
             ext[:, spare:] = jnp.zeros((padded, ext.shape[1] - spare), F32)
 
-    upper = 2 * position >= blocks
+    upper = position >= reach
     parity = jnp.where(upper, 1, 0)
+    final = jnp.where(upper, blocks - 1 - position, position)
+    final = jnp.where(final < reach, final, reach - 1)
     rank = [
-        jnp.where(parity == slot % 2, 4 + slot // 2, 1 + slot // 2) for slot in range(len(OFFSETS))
+        jnp.where(
+            parity == slot % 2,
+            1 + reach + lax.rem(slot // 2 + 2 * reach - 1 - final, reach),
+            1 + slot // 2,
+        )
+        for slot in range(len(OFFSETS))
     ] + [0]
     shifts = [rank[slot] - slot for slot in range(slots)]
 
@@ -219,11 +225,16 @@
     chunk = tangent.shape[0] // 2
     steps = 2 * (tangent.shape[1] // LANES)
     steps_ahead = jnp.where(first, jnp.where(side == 0, 3 * steps // 4, steps // 2), 0)
-
-    def prepare():
+    waits = (position >= 2) & (lax.rem(position, 2) == 0) & (position < blocks - 2)
+    steps_ahead = jnp.where(waits, jnp.where(side == 0, steps // 4, steps // 6), steps_ahead)
+    steps_far = jnp.where(first, steps, 7 * steps // 12)
+
+    def prepare_tangent():
         indices = moved(edges_on_edge_ref[...], edges, halo_edges, shifts)
         tangent_weight[...] = merged_weights(indices, eoe_weight_ref[...])
         edges_on_edge_ref[...] = indices
+
+    def prepare():
         indices = moved(cell_edges_ref[...], edges, halo_edges, shifts)
         diverge_weight[...] = merged_weights(indices, cell_weight_ref[...])
         cell_edges_ref[...] = indices
@@ -242,13 +253,15 @@
     def build_tangent(lower, higher):
         build(edges_on_edge_ref, tangent_weight, tangent, tangent_trail, chunk, lower, higher)
 
-    gather(order[:URGENT])
+    gather(order[:1])
     for load in loads[5:]:
         load.wait()
 
-    @pl.when(first)
+    pl.when(first)(prepare)
+
+    @pl.when(steps_ahead > 0)
     def _():
-        prepare()
+        prepare_tangent()
         build_tangent(0, steps_ahead)
 
     @pl.when(first)
@@ -262,14 +275,18 @@
             greeted = far_sem if offset > 0 else near_sem
             pl.when(later(slot))(functools.partial(signal, greeted, slot))
 
-    for slot in order[:URGENT]:
-        copy_of(slot).start()
-    gather(order[URGENT:])
-    for step, slot in enumerate(order[URGENT:], URGENT):
-        pl.when(step < slots - late)(copy_of(slot).start)
+    copy_of(order[0]).start()
+    for begin, end in ((1, reach), (reach, slots)):
+        gather(order[begin:end])
+        for step in range(begin, end):
+            if step < reach:
+                copy_of(order[step]).start()
+            else:
+                pl.when(step < slots - late)(copy_of(order[step]).start)
 
     pl.when(jnp.logical_not(first))(prepare)
-    build_tangent(steps_ahead, steps)
+    pl.when(steps_ahead == 0)(prepare_tangent)
+    build_tangent(steps_ahead, steps_far)
 
     @pl.when(first)
     def _():
@@ -282,8 +299,10 @@
     def _():
         pl.semaphore_wait(far_sem, greetings)
 
-    for step, slot in enumerate(order[URGENT:], URGENT):
-        pl.when(step >= slots - late)(copy_of(slot).start)
+    for step in range(reach, slots):
+        pl.when(step >= slots - late)(copy_of(order[step]).start)
+
+    build_tangent(steps_far, steps)
 
     ratio = jnp.zeros((1, cells), F32)
     below = jnp.zeros((1, cells), F32)
@@ -333,9 +352,17 @@
     tangent_sum[...] += tangent_part(edges, edges_near)
     average_sum[...] += average_part(cells, cells_near)
 
-    for pair in range(near - 1):
-        take(2 * pair + parity, near + pair)
-    averaged = average_sum[...] + average_part(cells_near, density_ext.shape[1])
+    def take_late(place):
+        take(2 * lax.rem(final + 1 + place, reach) + parity, near + place)
+
+    edges_late, cells_late = edges_near + 2 * halo_edges, cells_near + 2 * halo_cells
+    take_late(0)
+    take_late(1)
+    tangent_sum[...] += tangent_part(edges_near, edges_late)
+    average_sum[...] += average_part(cells_near, cells_late)
+
+    take_late(2)
+    averaged = average_sum[...] + average_part(cells_late, density_ext.shape[1])
     wind = wind_ext[...]
     fluxes = halves(jnp.concatenate([wind, wind], axis=0) * averaged)
     both = dot(fluxes, diverge[...])
@@ -346,7 +373,7 @@
     values[...] = (theta_ext[:, 0:cells] - STEP_SIZE * divergence[padded:])
     values[0:levels, :] = values[0:levels, :] * inverse[0:levels, :]
 
-    tangential = tangent_sum[...] + tangent_part(edges_near, wind_ext.shape[1])
+    tangential = tangent_sum[...] + tangent_part(edges_late, wind_ext.shape[1])
     tangential_ref[...] = tangential[0:levels]
 
     value = jnp.zeros((1, cells), F32)

time: 14.6 us -> 14.2 us (0.973)
  Pallas kernels: 13.8 us -> 13.4 us
    pallas_call x1, Pallas kernels: 13.1 us -> 12.7 us  [shards(): pl.pallas_call(kernel, out_shape=tuple((pltpu.VMEM((levels, width), F32)...]
where the time goes in v5:
time: 14.2 us; the launch traced here: 14 us
  Pallas kernels  13.4 us (94%)
  between operations  0.64 us (5%)
    pallas_call x1, Pallas kernels, shards(): pl.pallas_call(kernel, out_shape=tuple((pltpu.VMEM((levels, width), F32)...  12.7 us
    pallas_call x1, Pallas kernels, shards(): pl.pallas_call(deliver, out_shape=tuple((jax.ShapeDtypeStruct((levels, 1,...  0.73 us

profile of v5, /device:TPU:0, one launch (start us, length us, event | category | flops | bytes accessed | tf_op | source)
XLA Modules:
  0.0 14.0 jit_solution(4993106922081922512)
XLA Ops:
  0.6 12.7 %shard_map.130 = (f32[55,256]{1,0:T(8,128)S(1)}, f32[55,256]{1,0:T(8,128)S(1)}, f32[55,768]{1,0:T(8,128)S(1)}) custom-call(f32[55,1,768]{2,1,0:T(1,128)} %bitcast.13, f32[55,1,256]{2,1,0:T(1,128)} %bitcast.14, f32[55,1,256]{2,1,0:T(1,128)} %bitcast.15, s32[6,1,256]{2,1,0:T(1,128)} %bitcast.19, s32[1,2,1664]{2,1,0:T(2,128)} %edge_cells_hbm.1, ...), custom_call_target="tpu_custom_call" | custom-call | tf_op jit(solution)/shard_map/pallas_call | solution.py:418
  13.3 0.7 %shard_map.131 = (f32[55,1,256]{2,1,0:T(1,128)}, f32[55,1,256]{2,1,0:T(1,128)}, f32[55,1,768]{2,1,0:T(1,128)}) custom-call(f32[55,256]{1,0:T(8,128)S(1)} %get-tuple-element.9.refs_0_, f32[55,256]{1,0:T(8,128)S(1)} %get-tuple-element.10.refs_1_, f32[55,768]{1,0:T(8,128)S(1)} %get-tuple-element.11.refs_2_), custom_call_target="tpu_custom_call" | custom-call | tf_op jit(solution)/shard_map/pallas_call | solution.py:452

commit v6 on v5

--- a/solution.py
+++ b/solution.py
@@ -98,7 +98,7 @@
     average, average_weight, diverge, diverge_trail, diverge_weight,
     tangent, tangent_trail, tangent_weight,
     average_sum, tangent_sum, inverse, carried, ratios, values,
-    send_sem, recv_sem, load_sem, near_sem, far_sem,
+    recv_sem, load_sem, near_sem, far_sem,
 ):
     blocks = lax.axis_size("blk")
     position = lax.axis_index("blk")
@@ -216,7 +216,7 @@
         return pltpu.make_async_remote_copy(
             src_ref=send.at[slot],
             dst_ref=received.at[slot],
-            send_sem=send_sem.at[slot],
+            send_sem=load_sem.at[slot],
             recv_sem=recv_sem.at[slot],
             device_id=target(slot),
             device_id_type=pl.DeviceIdType.MESH,
@@ -304,19 +304,32 @@
 
     build_tangent(steps_far, steps)
 
-    ratio = jnp.zeros((1, cells), F32)
-    below = jnp.zeros((1, cells), F32)
-    for level in range(levels):
-        if level < levels - 1:
-            above = coupling_ref[level : level + 1, :]
-        else:
-            above = jnp.zeros((1, cells), F32)
-        reciprocal = 1.0 / (1.0 + below + above - below * ratio)
-        ratio = above * reciprocal
+    middle = levels // 2
+    none = jnp.zeros((1, cells), F32)
+
+    def interface(level):
+        return coupling_ref[level : level + 1, :] if 0 <= level < levels - 1 else none
+
+    def eliminate(level, came, ratio):
+        before, after = (interface(level - 1), interface(level))[:: 1 if came < 0 else -1]
+        reciprocal = 1.0 / (1.0 + before + after - before * ratio)
         inverse[level : level + 1, :] = reciprocal
-        carried[level : level + 1, :] = below * reciprocal
+        carried[level : level + 1, :] = before * reciprocal
+        ratio = after * reciprocal
         ratios[level : level + 1, :] = ratio
-        below = above
+        return ratio
+
+    upward, downward = none, none
+    for step in range(max(middle, levels - 1 - middle)):
+        if step < middle:
+            upward = eliminate(step, -1, upward)
+        if levels - 1 - step > middle:
+            downward = eliminate(levels - 1 - step, 1, downward)
+    before, after = interface(middle - 1), interface(middle)
+    reciprocal = 1.0 / (1.0 + before * (1.0 - upward) + after * (1.0 - downward))
+    inverse[middle : middle + 1, :] = reciprocal
+    carried[middle : middle + 1, :] = before * reciprocal
+    ratios[middle : middle + 1, :] = after * reciprocal
 
     def tangent_part(lower, higher):
         part = halves(wind_ext[:, lower:higher])
@@ -334,7 +347,6 @@
         return both[0 : 2 * padded] + both[2 * padded :]
 
     def take(slot, place):
-        copy_of(slot).wait_recv()
         start = cells + place * halo_cells
         density_ext[:, start : start + halo_cells] = received[slot, :, 0:halo_cells]
         theta_ext[:, start : start + halo_cells] = received[slot, :, halo_cells : 2 * halo_cells]
@@ -345,23 +357,26 @@
     average_sum[...] = average_part(0, cells)
 
     near = 1 + reach
-    take(slots - 1, 0)
-    for pair in range(near - 1):
-        take(2 * pair + 1 - parity, 1 + pair)
+    soon = [slots - 1] + [2 * pair + 1 - parity for pair in range(reach)]
+    for slot in soon:
+        copy_of(slot).wait_recv()
+    for place, slot in enumerate(soon):
+        take(slot, place)
     edges_near, cells_near = edges + near * halo_edges, cells + near * halo_cells
     tangent_sum[...] += tangent_part(edges, edges_near)
     average_sum[...] += average_part(cells, cells_near)
 
-    def take_late(place):
-        take(2 * lax.rem(final + 1 + place, reach) + parity, near + place)
-
+    slow = [2 * lax.rem(final + 1 + place, reach) + parity for place in range(reach)]
     edges_late, cells_late = edges_near + 2 * halo_edges, cells_near + 2 * halo_cells
-    take_late(0)
-    take_late(1)
+    for slot in slow[:2]:
+        copy_of(slot).wait_recv()
+    for place in range(2):
+        take(slow[place], near + place)
     tangent_sum[...] += tangent_part(edges_near, edges_late)
     average_sum[...] += average_part(cells_near, cells_late)
 
-    take_late(2)
+    copy_of(slow[2]).wait_recv()
+    take(slow[2], near + 2)
     averaged = average_sum[...] + average_part(cells_late, density_ext.shape[1])
     wind = wind_ext[...]
     fluxes = halves(jnp.concatenate([wind, wind], axis=0) * averaged)
@@ -376,15 +391,31 @@
     tangential = tangent_sum[...] + tangent_part(edges_late, wind_ext.shape[1])
     tangential_ref[...] = tangential[0:levels]
 
-    value = jnp.zeros((1, cells), F32)
-    for level in range(levels):
-        value = values[level : level + 1, :] + carried[level : level + 1, :] * value
-        values[level : level + 1, :] = value
-    theta_new_ref[levels - 1 : levels, :] = value
-    for level in range(levels - 2, -1, -1):
-        value = values[level : level + 1, :] + ratios[level : level + 1, :] * value
-        theta_new_ref[level : level + 1, :] = value
-
+    def row(ref, level):
+        return ref[level : level + 1, :]
+
+    upward, downward = none, none
+    for step in range(max(middle, levels - 1 - middle)):
+        if step < middle:
+            upward = row(values, step) + row(carried, step) * upward
+            values[step : step + 1, :] = upward
+        level = levels - 1 - step
+        if level > middle:
+            downward = row(values, level) + row(carried, level) * downward
+            values[level : level + 1, :] = downward
+    upward = (
+        row(values, middle) + row(carried, middle) * upward + row(ratios, middle) * downward
+    )
+    theta_new_ref[middle : middle + 1, :] = upward
+    downward = upward
+    for step in range(1, max(middle, levels - 1 - middle) + 1):
+        if middle - step >= 0:
+            upward = row(values, middle - step) + row(ratios, middle - step) * upward
+            theta_new_ref[middle - step : middle - step + 1, :] = upward
+        level = middle + step
+        if level < levels:
+            downward = row(values, level) + row(ratios, level) * downward
+            theta_new_ref[level : level + 1, :] = downward
     for slot in SEND_ORDER:
         copy_of(slot).wait_send()
 
@@ -442,7 +473,6 @@
             pltpu.VMEM((padded, cells), F32),
             pltpu.VMEM((padded, cells), F32),
             pltpu.SemaphoreType.DMA((slots,)),
-            pltpu.SemaphoreType.DMA((slots,)),
             pltpu.SemaphoreType.DMA((len(arguments),)),
             pltpu.SemaphoreType.REGULAR,
             pltpu.SemaphoreType.REGULAR,

time: 14.2 us -> 14 us (0.986)
  Pallas kernels: 13.4 us -> 13.2 us
    pallas_call x1, Pallas kernels: 12.7 us -> 12.5 us  [shards(): pl.pallas_call(kernel, out_shape=tuple((pltpu.VMEM((levels, width), F32)...]
where the time goes in v6:
time: 14 us; the launch traced here: 13.9 us
  Pallas kernels  13.2 us (94%)
  between operations  0.64 us (5%)
    pallas_call x1, Pallas kernels, shards(): pl.pallas_call(kernel, out_shape=tuple((pltpu.VMEM((levels, width), F32)...  12.5 us
    pallas_call x1, Pallas kernels, shards(): pl.pallas_call(deliver, out_shape=tuple((jax.ShapeDtypeStruct((levels, 1,...  0.73 us

profile of v6, /device:TPU:0, one launch (start us, length us, event | category | flops | bytes accessed | tf_op | source)
XLA Modules:
  0.0 13.9 jit_solution(7605240590546185908)
XLA Ops:
  0.6 12.5 %shard_map.130 = (f32[55,256]{1,0:T(8,128)S(1)}, f32[55,256]{1,0:T(8,128)S(1)}, f32[55,768]{1,0:T(8,128)S(1)}) custom-call(f32[55,1,768]{2,1,0:T(1,128)} %bitcast.13, f32[55,1,256]{2,1,0:T(1,128)} %bitcast.14, f32[55,1,256]{2,1,0:T(1,128)} %bitcast.15, s32[6,1,256]{2,1,0:T(1,128)} %bitcast.19, s32[1,2,1664]{2,1,0:T(2,128)} %edge_cells_hbm.1, ...), custom_call_target="tpu_custom_call" | custom-call | tf_op jit(solution)/shard_map/pallas_call | solution.py:449
  13.1 0.7 %shard_map.131 = (f32[55,1,256]{2,1,0:T(1,128)}, f32[55,1,256]{2,1,0:T(1,128)}, f32[55,1,768]{2,1,0:T(1,128)}) custom-call(f32[55,256]{1,0:T(8,128)S(1)} %get-tuple-element.9.refs_0_, f32[55,256]{1,0:T(8,128)S(1)} %get-tuple-element.10.refs_1_, f32[55,768]{1,0:T(8,128)S(1)} %get-tuple-element.11.refs_2_), custom_call_target="tpu_custom_call" | custom-call | tf_op jit(solution)/shard_map/pallas_call | solution.py:482

commit v7 on v6

--- a/solution.py
+++ b/solution.py
@@ -11,11 +11,13 @@
 OFFSETS = (1, -1, 2, -2, 3, -3)
 SEND_ORDER = (4, 5, 2, 3, 0, 1, 6)
 WRAP_ORDERS = {
-    -1: (0, 2, 4, 5, 3, 1, 6),
-    -2: (2, 4, 5, 3, 0, 1, 6),
-    0: (4, 2, 0, 6, 1, 3, 5),
-    1: (1, 4, 2, 0, 6, 3, 5),
-    2: (3, 1, 4, 2, 0, 6, 5),
+    (-1, None): (0, 2, 4, 5, 3, 1, 6),
+    (-2, None): (2, 4, 5, 3, 0, 1, 6),
+    (0, None): (4, 2, 0, 6, 1, 3, 5),
+    (1, 0): (1, 4, 2, 0, 6, 5, 3),
+    (1, 1): (1, 4, 2, 0, 6, 3, 5),
+    (2, None): (3, 1, 4, 2, 0, 6, 5),
+    (3, None): (5, 3, 2, 0, 4, 1, 6),
 }
 LANES = 128
 PACKED = 16
@@ -146,6 +148,7 @@
     first = position == 0
     waits_far = jnp.where(first, 0, jnp.maximum(reach - position, 0))
     late = jnp.where(first, reach + 1, waits_far)
+    holds = position == reach
 
     def signal(semaphore, slot):
         pl.semaphore_signal(
@@ -189,8 +192,11 @@
 
     order = []
     for step, slot in enumerate(SEND_ORDER):
-        for place, slots_there in WRAP_ORDERS.items():
-            slot = jnp.where(position == lax.rem(place + blocks, blocks), slots_there[step], slot)
+        for (place, way), slots_there in WRAP_ORDERS.items():
+            here = position == lax.rem(place + blocks, blocks)
+            if way is not None:
+                here = here & (side == way)
+            slot = jnp.where(here, slots_there[step], slot)
         order.append(slot)
 
     edge_rows = lax.broadcasted_iota(jnp.int32, (edges, halo_edges), 0)
@@ -224,9 +230,10 @@
 
     chunk = tangent.shape[0] // 2
     steps = 2 * (tangent.shape[1] // LANES)
-    steps_ahead = jnp.where(first, jnp.where(side == 0, 3 * steps // 4, steps // 2), 0)
-    waits = (position >= 2) & (lax.rem(position, 2) == 0) & (position < blocks - 2)
-    steps_ahead = jnp.where(waits, jnp.where(side == 0, steps // 4, steps // 6), steps_ahead)
+    steps_ahead = jnp.where(
+        first, jnp.where(side == 0, 7 * steps // 12, steps // 4), 0
+    )
+    waits = (lax.rem(position, 2) == 0) & (position < blocks - 2)
     steps_far = jnp.where(first, steps, 7 * steps // 12)
 
     def prepare_tangent():
@@ -234,10 +241,7 @@
         tangent_weight[...] = merged_weights(indices, eoe_weight_ref[...])
         edges_on_edge_ref[...] = indices
 
-    def prepare():
-        indices = moved(cell_edges_ref[...], edges, halo_edges, shifts)
-        diverge_weight[...] = merged_weights(indices, cell_weight_ref[...])
-        cell_edges_ref[...] = indices
+    def prepare_average():
         indices = moved(edge_cells_ref[...], cells, halo_cells, shifts)
         edge_cells_ref[:, 0:edges] = indices[:, 0:edges]
         for slot in range(slots):
@@ -248,6 +252,11 @@
             edge_cells_ref[...], jnp.full(edge_cells_ref.shape, 0.5, F32)
         )
         build(edge_cells_ref, average_weight, average, None, average.shape[0])
+
+    def prepare_diverge():
+        indices = moved(cell_edges_ref[...], edges, halo_edges, shifts)
+        diverge_weight[...] = merged_weights(indices, cell_weight_ref[...])
+        cell_edges_ref[...] = indices
         build(cell_edges_ref, diverge_weight, diverge, diverge_trail, chunk)
 
     def build_tangent(lower, higher):
@@ -257,7 +266,9 @@
     for load in loads[5:]:
         load.wait()
 
-    pl.when(first)(prepare)
+    pl.when(waits)(functools.partial(gather, order[1:]))
+    pl.when(first)(prepare_average)
+    pl.when(first)(prepare_diverge)
 
     @pl.when(steps_ahead > 0)
     def _():
@@ -277,14 +288,22 @@
 
     copy_of(order[0]).start()
     for begin, end in ((1, reach), (reach, slots)):
-        gather(order[begin:end])
+        pl.when(jnp.logical_not(waits))(functools.partial(gather, order[begin:end]))
         for step in range(begin, end):
             if step < reach:
                 copy_of(order[step]).start()
             else:
-                pl.when(step < slots - late)(copy_of(order[step]).start)
-
-    pl.when(jnp.logical_not(first))(prepare)
+                now = (step < slots - late) & jnp.logical_not(holds)
+                pl.when(now)(copy_of(order[step]).start)
+
+    pl.when(jnp.logical_not(first))(prepare_average)
+
+    @pl.when(holds)
+    def _():
+        for slot in order[reach:]:
+            copy_of(slot).start()
+
+    pl.when(jnp.logical_not(first))(prepare_diverge)
     pl.when(steps_ahead == 0)(prepare_tangent)
     build_tangent(steps_ahead, steps_far)
 

time: 14 us -> 14 us (level)
  no operation moved by 1% of the time
where the time goes in v7:
time: 14 us; the launch traced here: 13.8 us
  Pallas kernels  13.2 us (94%)
  between operations  0.64 us (5%)
    pallas_call x1, Pallas kernels, shards(): pl.pallas_call(kernel, out_shape=tuple((pltpu.VMEM((levels, width), F32)...  12.5 us
    pallas_call x1, Pallas kernels, shards(): pl.pallas_call(deliver, out_shape=tuple((jax.ShapeDtypeStruct((levels, 1,...  0.73 us

profile of v7, /device:TPU:0, one launch (start us, length us, event | category | flops | bytes accessed | tf_op | source)
XLA Modules:
  0.0 13.8 jit_solution(3842062636383243157)
XLA Ops:
  0.6 12.5 %shard_map.130 = (f32[55,256]{1,0:T(8,128)S(1)}, f32[55,256]{1,0:T(8,128)S(1)}, f32[55,768]{1,0:T(8,128)S(1)}) custom-call(f32[55,1,768]{2,1,0:T(1,128)} %bitcast.13, f32[55,1,256]{2,1,0:T(1,128)} %bitcast.14, f32[55,1,256]{2,1,0:T(1,128)} %bitcast.15, s32[6,1,256]{2,1,0:T(1,128)} %bitcast.19, s32[1,2,1664]{2,1,0:T(2,128)} %edge_cells_hbm.1, ...), custom_call_target="tpu_custom_call" | custom-call | tf_op jit(solution)/shard_map/pallas_call | solution.py:468
  13.1 0.7 %shard_map.131 = (f32[55,1,256]{2,1,0:T(1,128)}, f32[55,1,256]{2,1,0:T(1,128)}, f32[55,1,768]{2,1,0:T(1,128)}) custom-call(f32[55,256]{1,0:T(8,128)S(1)} %get-tuple-element.9.refs_0_, f32[55,256]{1,0:T(8,128)S(1)} %get-tuple-element.10.refs_1_, f32[55,768]{1,0:T(8,128)S(1)} %get-tuple-element.11.refs_2_), custom_call_target="tpu_custom_call" | custom-call | tf_op jit(solution)/shard_map/pallas_call | solution.py:501

commit v8 on v7

--- a/solution.py
+++ b/solution.py
@@ -123,8 +123,8 @@
 
     loads = (
         (send_edges_hbm, send_edges_ref),
+        (send_cells_hbm, send_cells_ref),
         (wind_hbm, wind_ref),
-        (send_cells_hbm, send_cells_ref),
         (density_hbm, density_ref),
         (theta_hbm, theta_ref),
         (edge_cells_hbm, edge_cells_ref),
@@ -164,17 +164,11 @@
     for slot in SEND_ORDER:
         pl.when(jnp.logical_not(later(slot)))(functools.partial(signal, barrier, slot))
 
-    for load in loads[:5]:
-        load.wait()
-    for ext, ref in ((wind_ext, wind_ref), (density_ext, density_ref), (theta_ext, theta_ref)):
+    def keep(ext, ref):
         owned = ref.shape[1]
         ext[0:levels, 0:owned] = ref[...]
         if levels < padded:
             ext[levels:padded, 0:owned] = jnp.zeros((padded - levels, owned), F32)
-    spare = cells + slots * halo_cells
-    for ext in (density_ext, theta_ext):
-        if spare < ext.shape[1]:
-            ext[:, spare:] = jnp.zeros((padded, ext.shape[1] - spare), F32)
 
     upper = position >= reach
     parity = jnp.where(upper, 1, 0)
@@ -202,21 +196,33 @@
     edge_rows = lax.broadcasted_iota(jnp.int32, (edges, halo_edges), 0)
     cell_rows = lax.broadcasted_iota(jnp.int32, (cells, halo_cells), 0)
 
+    def edge_picks(slot):
+        return jnp.where(edge_rows == send_edges_ref[pl.ds(slot, 1), :], 1.0, 0.0).astype(BF16)
+
+    def cell_picks(slot):
+        return jnp.where(cell_rows == send_cells_ref[pl.ds(slot, 1), :], 1.0, 0.0).astype(BF16)
+
+    def own_wind():
+        return halves(wind_ext[:, 0:edges])
+
+    def own_cells():
+        return halves(
+            jnp.concatenate([density_ext[:, 0:cells], theta_ext[:, 0:cells]], axis=0)
+        )
+
+    def pack_wind(slot, both):
+        send[slot, :, 2 * halo_cells :] = both[0:padded] + both[padded:]
+
+    def pack_cells(slot, both):
+        both = both[0 : 2 * padded] + both[2 * padded :]
+        send[slot, :, 0:halo_cells] = both[0:padded]
+        send[slot, :, halo_cells : 2 * halo_cells] = both[padded:]
+
     def gather(some):
-        wind_own = halves(wind_ext[:, 0:edges])
-        cells_own = halves(
-            jnp.concatenate([density_ext[:, 0:cells], theta_ext[:, 0:cells]], axis=0)
-        )
+        wind_own, cells_own = own_wind(), own_cells()
         for slot in some:
-            row = pl.ds(slot, 1)
-            picks = jnp.where(edge_rows == send_edges_ref[row, :], 1.0, 0.0).astype(BF16)
-            both = dot(wind_own, picks)
-            send[slot, :, 2 * halo_cells :] = both[0:padded] + both[padded:]
-            picks = jnp.where(cell_rows == send_cells_ref[row, :], 1.0, 0.0).astype(BF16)
-            both = dot(cells_own, picks)
-            both = both[0 : 2 * padded] + both[2 * padded :]
-            send[slot, :, 0:halo_cells] = both[0:padded]
-            send[slot, :, halo_cells : 2 * halo_cells] = both[padded:]
+            pack_wind(slot, dot(wind_own, edge_picks(slot)))
+            pack_cells(slot, dot(cells_own, cell_picks(slot)))
 
     def copy_of(slot):
         return pltpu.make_async_remote_copy(
@@ -262,7 +268,20 @@
     def build_tangent(lower, higher):
         build(edges_on_edge_ref, tangent_weight, tangent, tangent_trail, chunk, lower, higher)
 
-    gather(order[:1])
+    for load in loads[:2]:
+        load.wait()
+    picks = edge_picks(order[0]), cell_picks(order[0])
+    for load in loads[2:5]:
+        load.wait()
+    keep(wind_ext, wind_ref)
+    keep(density_ext, density_ref)
+    keep(theta_ext, theta_ref)
+    pack_wind(order[0], dot(own_wind(), picks[0]))
+    pack_cells(order[0], dot(own_cells(), picks[1]))
+    spare = cells + slots * halo_cells
+    for ext in (density_ext, theta_ext):
+        if spare < ext.shape[1]:
+            ext[:, spare:] = jnp.zeros((padded, ext.shape[1] - spare), F32)
     for load in loads[5:]:
         load.wait()
 

time: 14 us -> 14 us (level)
  no operation moved by 1% of the time
where the time goes in v8:
time: 14 us; the launch traced here: 13.8 us
  Pallas kernels  13.2 us (94%)
  between operations  0.64 us (5%)
    pallas_call x1, Pallas kernels, shards(): pl.pallas_call(kernel, out_shape=tuple((pltpu.VMEM((levels, width), F32)...  12.4 us
    pallas_call x1, Pallas kernels, shards(): pl.pallas_call(deliver, out_shape=tuple((jax.ShapeDtypeStruct((levels, 1,...  0.73 us

profile of v8, /device:TPU:0, one launch (start us, length us, event | category | flops | bytes accessed | tf_op | source)
XLA Modules:
  0.0 13.8 jit_solution(7367511371851030310)
XLA Ops:
  0.6 12.4 %shard_map.130 = (f32[55,256]{1,0:T(8,128)S(1)}, f32[55,256]{1,0:T(8,128)S(1)}, f32[55,768]{1,0:T(8,128)S(1)}) custom-call(f32[55,1,768]{2,1,0:T(1,128)} %bitcast.13, f32[55,1,256]{2,1,0:T(1,128)} %bitcast.14, f32[55,1,256]{2,1,0:T(1,128)} %bitcast.15, s32[6,1,256]{2,1,0:T(1,128)} %bitcast.19, s32[1,2,1664]{2,1,0:T(2,128)} %edge_cells_hbm.1, ...), custom_call_target="tpu_custom_call" | custom-call | tf_op jit(solution)/shard_map/pallas_call | solution.py:487
  13.1 0.7 %shard_map.131 = (f32[55,1,256]{2,1,0:T(1,128)}, f32[55,1,256]{2,1,0:T(1,128)}, f32[55,1,768]{2,1,0:T(1,128)}) custom-call(f32[55,256]{1,0:T(8,128)S(1)} %get-tuple-element.9.refs_0_, f32[55,256]{1,0:T(8,128)S(1)} %get-tuple-element.10.refs_1_, f32[55,768]{1,0:T(8,128)S(1)} %get-tuple-element.11.refs_2_), custom_call_target="tpu_custom_call" | custom-call | tf_op jit(solution)/shard_map/pallas_call | solution.py:520
